TPU v7x, 32 devices: a whole 2x2x4 slice. The times are simulated.
32 devices in a mesh: rep: 2 (over y), seq: 4 (over z), head: 2 (over x), sub: 2 (over core).
Axes of the slice: x: 2, y: 2, z: 4, core: 2. Of those that a mesh axis runs over, the one named last changes fastest.
Arguments:
- tokens: bfloat16 [32, 4096], P(('rep', 'sub'), 'seq'), parts along dimension 0, may hold values from -260 to 260
- attn_gain: float32 [4096], P('seq'), may hold values from 0.1 to 1.9
- w_query: bfloat16 [4096, 4096], P('seq', 'head'), may hold values from -0.09375 to 0.09375
- key_projection_weight: bfloat16 [4096, 1024], P('seq', 'head'), may hold values from -0.375 to 0.375
- value_projection_weight: bfloat16 [4096, 1024], P('seq', 'head'), may hold values from -0.375 to 0.375
- w_attn_out: bfloat16 [4096, 4096], P('head', 'seq'), may hold values from -0.09375 to 0.09375
- cache_keys: bfloat16 [32, 8, 2048, 128], P(('rep', 'sub'), 'head', 'seq'), parts along dimension 0, may hold values from -2500 to 2500
- stored_value_cache: bfloat16 [32, 8, 2048, 128], P(('rep', 'sub'), 'head', 'seq'), parts along dimension 0, may hold values from -12 to 12
- lengths: int32 [32], P(('rep', 'sub')), parts along dimension 0, may hold values from 1024 to 2048
- positions: int32 [32], P(('rep', 'sub')), parts along dimension 0, may hold values from 0 to 2047
- mamba_gain: float32 [4096], replicated, may hold values from 0.1 to 1.9
- w_in: bfloat16 [2, 4096, 8192], P(None, None, ('seq', 'head')), may hold values from -0.09375 to 0.09375
- conv_weight: float32 [4, 8192], P(None, ('seq', 'head')), may hold values from -3 to 3
- conv_bias: float32 [8192], P(('seq', 'head')), may hold values from -0.5 to 0.5
- conv_state: float32 [32, 3, 8192], P(('rep', 'sub'), None, ('seq', 'head')), parts along dimension 0, may hold values from -6 to 6
- w_xproj: bfloat16 [8192, 288], P(('seq', 'head')), may hold values from -0.0625 to 0.0625
- w_dt: bfloat16 [256, 8192], P(None, ('seq', 'head')), may hold values from -0.375 to 0.375
- dt_bias: float32 [8192], P(('seq', 'head')), may hold values from -4 to 0
- a_log: float32 [16, 8192], P(None, ('seq', 'head')), may hold values from 0 to 2.77
- skip_gain: float32 [8192], P(('seq', 'head')), may hold values from 0.25 to 2
- ssm_state: float32 [32, 16, 8192], P(('rep', 'sub'), None, ('seq', 'head')), parts along dimension 0, may hold values from -6 to 6
- w_mamba_out: bfloat16 [8192, 4096], P(('seq', 'head')), may hold values from -0.09375 to 0.09375
Outputs:
- hidden_out: bfloat16 [32, 4096], P(('rep', 'sub'), 'seq'), parts along dimension 0
- new_state: float32 [32, 16, 8192], P(('rep', 'sub'), None, ('seq', 'head')), parts along dimension 0
There are 2 independent parts, one for each index of `rep`. A program takes and returns all parts, laid end to end along the dimension named above; an argument that names none is the same for every part. Nothing has to cross between parts.
Inputs may be any that keep to these rules, and one draw needn't show every extreme that they name: Cache positions p < lengths[b] hold sequence b's past keys and values; later positions are not attended.
All inputs are finite; a program needn't handle non-finite values.
Results may differ from a plain program's by a relative error of at most 0.015.
Values may be sent and summed in bfloat16 or wider, within the bound.
A program may use at most 128 MiB of HBM per device.

v0:
```python
import math
import jax
import jax.numpy as jnp
from jax import lax
from jax.sharding import PartitionSpec as P

norm_eps = 1e-05
masked_floor = -1e30
rope_base = 10000.0


def joined(value, axis, join):
    pieces = jax.tree.map(lambda part: lax.all_gather(part, axis), value)
    head = jax.tree.map(lambda part: part[0], pieces)
    tail = jax.tree.map(lambda part: part[1:], pieces)
    subtotal, _ = lax.scan(lambda subtotal, section: (join(subtotal, section), None), head, tail)
    return subtotal


def apply_rotary(vectors, positions):
    half_dim = vectors.shape[-1] // 2
    frequency = jnp.exp(
        -math.log(rope_base) * 2.0 * jnp.arange(half_dim, dtype=jnp.float32) / (2 * half_dim)
    )
    angles = positions.astype(jnp.float32)[:, None] * frequency[None, :]
    cosine = jnp.cos(angles)[:, None, :]
    sine_part = jnp.sin(angles)[:, None, :]
    first_half = vectors[..., :half_dim]
    second_half = vectors[..., half_dim:]
    return jnp.concatenate(
        [
            first_half * cosine - second_half * sine_part,
            second_half * cosine + first_half * sine_part,
        ],
        axis=-1,
    )


def join_partial(earlier, later):
    max_one, sum_one, acc_one = earlier
    max_two, sum_two, acc_two = later
    joined_max = jnp.maximum(max_one, max_two)
    factor_one = jnp.exp(max_one - joined_max)
    factor_two = jnp.exp(max_two - joined_max)
    return (
        joined_max,
        sum_one * factor_one + sum_two * factor_two,
        acc_one * factor_one[..., None] + acc_two * factor_two[..., None],
    )


def local(
    tokens,
    attn_gain,
    w_query,
    key_projection_weight,
    value_projection_weight,
    w_attn_out,
    cache_keys,
    stored_value_cache,
    lengths,
    positions,
    mamba_gain,
    w_in,
    conv_weight,
    conv_bias,
    conv_state,
    w_xproj,
    w_dt,
    dt_bias,
    a_log,
    skip_gain,
    ssm_state,
    w_mamba_out,
):
    batch_rows = tokens.shape[0]
    feature_cols = tokens.shape[1]
    head_dim = cache_keys.shape[3]
    kv_local = cache_keys.shape[1]
    ctx_local = cache_keys.shape[2]
    q_local = w_query.shape[1] // head_dim
    query_group_count = q_local // kv_local
    model_width = feature_cols * lax.axis_size("seq")
    token_float = tokens.astype(jnp.float32)
    lifted = (token_float * attn_gain[None, :]).astype(jnp.bfloat16)
    part_query = jnp.dot(lifted, w_query, preferred_element_type=jnp.float32)
    part_key = jnp.dot(lifted, key_projection_weight, preferred_element_type=jnp.float32)
    part_value = jnp.dot(lifted, value_projection_weight, preferred_element_type=jnp.float32)
    squares = jnp.sum(token_float * token_float, axis=1)
    sum_squares = lax.psum(squares, "seq")
    part_query, part_key, part_value = lax.psum((part_query, part_key, part_value), "seq")
    inv_rms = lax.rsqrt(sum_squares / model_width + norm_eps)
    query_vectors = apply_rotary(
        (part_query * inv_rms[:, None]).reshape(batch_rows, q_local, head_dim), positions
    ).astype(jnp.bfloat16)
    fresh_key_rows = apply_rotary(
        (part_key * inv_rms[:, None]).reshape(batch_rows, kv_local, head_dim), positions
    ).astype(jnp.bfloat16)
    fresh_value_rows = (
        (part_value * inv_rms[:, None]).reshape(batch_rows, kv_local, head_dim).astype(jnp.bfloat16)
    )
    grouped_queries = query_vectors.reshape(batch_rows, kv_local, query_group_count, head_dim)
    score_scale = head_dim ** (-0.5)
    scores = (
        jnp.einsum(
            "bhgd,bhtd->bhgt", grouped_queries, cache_keys, preferred_element_type=jnp.float32
        )
        * score_scale
    )
    slot_index = lax.axis_index("seq") * ctx_local + jnp.arange(ctx_local, dtype=jnp.int32)
    live_mask = slot_index[None, None, None, :] < lengths[:, None, None, None]
    local_max = jnp.max(jnp.where(live_mask, scores, masked_floor), axis=-1)
    weights = jnp.where(live_mask, jnp.exp(scores - local_max[..., None]), 0.0)
    local_sum = jnp.sum(weights, axis=-1)
    local_acc = jnp.einsum(
        "bhgt,bhtd->bhgd",
        weights.astype(jnp.bfloat16),
        stored_value_cache,
        preferred_element_type=jnp.float32,
    )
    merged_max, merged_sum, merged_acc = joined(
        (local_max, local_sum, local_acc), "seq", join_partial
    )
    score_new = (
        jnp.einsum(
            "bhgd,bhd->bhg", grouped_queries.astype(jnp.float32), fresh_key_rows.astype(jnp.float32)
        )
        * score_scale
    )
    row_max = jnp.maximum(merged_max, score_new)
    old_factor = jnp.exp(merged_max - row_max)
    new_weight = jnp.exp(score_new - row_max)
    total_weight = merged_sum * old_factor + new_weight
    attended = (
        merged_acc * old_factor[..., None]
        + new_weight[..., None] * fresh_value_rows.astype(jnp.float32)[:, :, None, :]
    )
    attn_rows = (
        (attended / total_weight[..., None])
        .reshape(batch_rows, q_local * head_dim)
        .astype(jnp.bfloat16)
    )
    out_part = jnp.dot(attn_rows, w_attn_out, preferred_element_type=jnp.float32)
    summed = lax.psum(out_part, "head")
    mid_stream = (token_float + summed).astype(jnp.bfloat16)
    full_tokens = lax.all_gather(mid_stream, "seq", axis=1, tiled=True)
    full_float = full_tokens.astype(jnp.float32)
    inv_rms_two = lax.rsqrt(jnp.mean(full_float * full_float, axis=1) + norm_eps)
    lifted_two = (full_float * inv_rms_two[:, None] * mamba_gain[None, :]).astype(jnp.bfloat16)
    inner = jnp.dot(lifted_two, w_in[0], preferred_element_type=jnp.float32)
    gate_branch = jnp.dot(lifted_two, w_in[1], preferred_element_type=jnp.float32)
    window = jnp.concatenate([conv_state, inner[:, None, :]], axis=1)
    mixed = jnp.sum(window * conv_weight[None, :, :], axis=1) + conv_bias[None, :]
    activated = jax.nn.silu(mixed)
    proj_part = jnp.dot(activated.astype(jnp.bfloat16), w_xproj, preferred_element_type=jnp.float32)
    projected = lax.psum(proj_part, ("seq", "head"))
    rank_width = w_dt.shape[0]
    state_width = ssm_state.shape[1]
    dt_low = projected[:, :rank_width].astype(jnp.bfloat16)
    input_map = projected[:, rank_width : rank_width + state_width]
    output_map = projected[:, rank_width + state_width :]
    step_size = jax.nn.softplus(
        jnp.dot(dt_low, w_dt, preferred_element_type=jnp.float32) + dt_bias[None, :]
    )
    decay = jnp.exp(step_size[:, None, :] * (-jnp.exp(a_log))[None, :, :])
    new_state = decay * ssm_state + (step_size * activated)[:, None, :] * input_map[:, :, None]
    readout = jnp.sum(output_map[:, :, None] * new_state, axis=1) + skip_gain[None, :] * activated
    gated = (readout * jax.nn.silu(gate_branch)).astype(jnp.bfloat16)
    mamba_part = jnp.dot(gated, w_mamba_out, preferred_element_type=jnp.float32)
    share = lax.psum_scatter(
        mamba_part.astype(jnp.bfloat16), "seq", scatter_dimension=1, tiled=True
    ).astype(jnp.float32)
    share = lax.psum(share, "head")
    hidden_out = (mid_stream.astype(jnp.float32) + share).astype(jnp.bfloat16)
    return (hidden_out, new_state)


def solution(mesh):
    in_specs = (
        P(("rep", "sub"), "seq"),
        P("seq"),
        P("seq", "head"),
        P("seq", "head"),
        P("seq", "head"),
        P("head", "seq"),
        P(("rep", "sub"), "head", "seq", None),
        P(("rep", "sub"), "head", "seq", None),
        P(("rep", "sub")),
        P(("rep", "sub")),
        P(),
        P(None, None, ("seq", "head")),
        P(None, ("seq", "head")),
        P(("seq", "head")),
        P(("rep", "sub"), None, ("seq", "head")),
        P(("seq", "head"), None),
        P(None, ("seq", "head")),
        P(("seq", "head")),
        P(None, ("seq", "head")),
        P(("seq", "head")),
        P(("rep", "sub"), None, ("seq", "head")),
        P(("seq", "head"), None),
    )
    out_specs = (P(("rep", "sub"), "seq"), P(("rep", "sub"), None, ("seq", "head")))
    return jax.shard_map(local, mesh=mesh, in_specs=in_specs, out_specs=out_specs, check_vma=False)
```

profile of v0, /device:TPU:0, one launch (start us, length us, event | category | flops | bytes accessed | tf_op | source)
XLA Modules:
  0.0 205.1 jit_solution(17046458614477309599)
XLA Ops:
  7.3 3.6 %fusion.46 = f32[8,2048]{1,0:T(8,128)} fusion(bf16[1024,2048]{1,0:T(8,128)(2,1)} %param.26, bf16[8,1024]{1,0:T(8,128)(2,1)} %param.24, f32[1024]{0:T(1024)} %param.25), kind=kOutput, calls=%fused_computation.68 | convolution fusion | flops 33579008 | bytes 4280320 | tf_op jit(solution)/shard_map/dot_general | solution.py:86
  11.0 0.1 fusion.25
  11.2 0.2 fusion.44
  11.4 0.2 fusion.42
  11.7 21.4 %all-reduce = (f32[8]{0:T(128)S(1)}, f32[8,512]{1,0:T(8,128)S(1)}, f32[8,512]{1,0:T(8,128)S(1)}) all-reduce(f32[8]{0:T(128)S(1)} %fusion.25, f32[8,512]{1,0:T(8,128)S(1)} %fusion.44, f32[8,512]{1,0:T(8,128)S(1)} %fusion.42), channel_id=1, replica_groups=mesh['rep'=2,'seq'=4,'head'=2,'sub'=2] {'seq'}, use_global_device_ids=true, to_apply=%region_2.0 | all-reduce | flops 8200 | bytes 65600 | tf_op jit(solution)/shard_map/psum | solution.py:90
  33.3 0.1 multiply_cosine_fusion
  33.6 14.7 %all-reduce.3.cloned.1.call-done = f32[8,2048]{1,0:T(8,128)} async-done(((f32[8,2048]{1,0:T(8,128)}), f32[8,2048]{1,0:T(8,128)}) %all-reduce.3.cloned.1.call-update) | async-done | bytes 65552 | tf_op jit(solution)/shard_map/psum | solution.py:91
  48.3 1.1 multiply_bitcast_fusion
  49.4 0.1 subtract_convert_fusion
  49.5 3.6 %select_reduce_fusion = (f32[8,4,4]{2,1,0:T(4,128)S(1)}, f32[8,4,4,512]{3,2,1,0:T(4,128)S(1)}) fusion(pred[8,512]{1,0:T(8,128)(4,1)S(1)} %broadcast_compare_fusion, bf16[8,4,512,128]{3,2,1,0:T(8,128)(2,1)} %param.30, bf16[8,4,4,64]{3,2,1,0:T(4,128)(2,1)S(1)} %bitcast.72, bf16[8,4,4,64]{3,2,1,0:T(4,128)(2,1)S(1)} %bitcast.70), kind=kOutput, calls=%fused_computation.21 | convolution fusion | flops 17039232 | bytes 4493824 | tf_op jit(solution)/shard_map/bhgd,bhtd->bhgt/dot_general | solution.py:105
  53.1 13.1 %all-gather = f32[32,4,4]{2,1,0:T(4,128)S(1)} all-gather(f32[8,4,4]{2,1,0:T(4,128)S(1)} %get-tuple-element.94), channel_id=2, replica_groups=mesh['rep'=2,'seq'=4,'head'=2,'sub'=2] {'seq'}, dimensions={0}, use_global_device_ids=true | all-gather | bytes 2560 | tf_op jit(solution)/shard_map/all_gather | solution.py:13
  66.2 0.3 fusion.13
  66.5 13.2 %all-gather.1 = f32[32,4,4]{2,1,0:T(4,128)S(1)} all-gather(f32[8,4,4]{2,1,0:T(4,128)S(1)} %fusion.13), channel_id=3, replica_groups=mesh['rep'=2,'seq'=4,'head'=2,'sub'=2] {'seq'}, dimensions={0}, use_global_device_ids=true | all-gather | bytes 2560 | tf_op jit(solution)/shard_map/all_gather | solution.py:13
  79.7 0.7 fusion.17
  80.4 13.9 %all-gather.2 = f32[32,4,4,128]{3,2,1,0:T(4,128)S(1)} all-gather(f32[8,4,4,128]{3,2,1,0:T(4,128)S(1)} %fusion.17), channel_id=4, replica_groups=mesh['rep'=2,'seq'=4,'head'=2,'sub'=2] {'seq'}, dimensions={0}, use_global_device_ids=true | all-gather | bytes 327680 | tf_op jit(solution)/shard_map/all_gather | solution.py:13
  94.3 0.2 fusion.37
  94.6 0.1 copy.59
  94.7 0.1 copy.50
  94.8 0.2 copy.52
  94.9 0.1 copy.51
  95.0 0.2 copy.53
  95.2 1.5 while.14
  95.2 0.1 copy.68
  95.3 0.1 copy.69
  95.4 0.2 fusion.73
  95.7 0.1 copy.68
  95.8 0.1 copy.69
  95.9 0.2 fusion.73
  96.2 0.1 copy.68
  96.3 0.1 copy.69
  96.4 0.2 fusion.73
  96.7 0.1 copy.57
  96.8 0.1 copy.54
  96.9 0.1 copy.55
  97.0 0.2 fusion.23
  97.2 2.8 %fusion.59 = f32[8,1024]{1,0:T(8,128)S(1)} fusion(bf16[8,2048]{1,0:T(8,128)(2,1)S(1)} %convert_element_type.78, bf16[2048,1024]{1,0:T(8,128)(2,1)} %param.29), kind=kOutput, calls=%fused_computation.88 | convolution fusion | flops 33554432 | bytes 4259840 | tf_op jit(solution)/shard_map/dot_general | solution.py:143
  100.0 8.3 %psum.53 = f32[8,1024]{1,0:T(8,128)S(1)} all-reduce(f32[8,1024]{1,0:T(8,128)S(1)} %fusion.59), channel_id=1, replica_groups=mesh['rep'=2,'seq'=4,'head'=2,'sub'=2] {'head'}, use_global_device_ids=true, to_apply=%region_9.10 | all-reduce | flops 8192 | bytes 65536 | tf_op jit(solution)/shard_map/psum | solution.py:144
  108.4 13.1 %all_gather.27 = bf16[8,4096]{1,0:T(8,128)(2,1)S(1)} all-gather(bf16[8,1024]{1,0:T(8,128)(2,1)S(1)} %fusion.26), channel_id=1, replica_groups=mesh['rep'=2,'seq'=4,'head'=2,'sub'=2] {'seq'}, dimensions={1}, use_global_device_ids=true | all-gather | bytes 81920 | tf_op jit(solution)/shard_map/all_gather | solution.py:146
  121.5 0.1 fusion.14
  121.8 4.7 %fusion.9 = f32[8,1,1024]{2,0,1:T(8,128)S(1)} fusion(bf16[2,4096,1024]{2,1,0:T(8,128)(2,1)} %param.35, bf16[8,4096]{1,0:T(8,128)(2,1)S(1)} %all_gather.27, f32[4096]{0:T(1024)S(1)} %copy-done.9, f32[8]{0:T(128)S(1)} %add_rsqrt_fusion), kind=kOutput, calls=%fused_computation.16 | convolution fusion | flops 67239936 | bytes 8503328 | tf_op jit(solution)/shard_map/dot_general | solution.py:150
  126.5 0.3 fusion.34
  126.8 35.1 %psum.54 = f32[8,288]{1,0:T(8,128)S(1)} all-reduce(f32[8,288]{1,0:T(8,128)S(1)} %fusion.34), channel_id=1, replica_groups=mesh['rep'=2,'seq'=4,'head'=2,'sub'=2] {'seq','head'}, use_global_device_ids=true, to_apply=%region_12.13 | all-reduce | flops 2304 | bytes 18432 | tf_op jit(solution)/shard_map/psum | solution.py:156
  162.0 0.2 fusion.54
  162.2 1.0 multiply_reduce_fusion
  163.2 8.7 %convolution_convert_fusion = bf16[8,4096]{1,0:T(8,128)(2,1)} fusion(bf16[1024,4096]{1,0:T(8,128)(2,1)} %param.45, bf16[2,4096,1024]{2,1,0:T(8,128)(2,1)} %param.35, f32[8,1024]{1,0:T(8,128)S(1)} %get-tuple-element.79, f32[1024]{0:T(1024)S(1)} %copy-done.14, bf16[8,4096]{1,0:T(8,128)(2,1)S(1)} %all_gather.27, f32[4096]{0:T(1024)S(1)} %copy-done.9, ...), kind=kOutput, calls=%fused_computation.14 | convolution fusion | flops 134488064 | bytes 16998432 | tf_op jit(solution)/shard_map/dot_general | solution.py:169
  172.0 16.6 %reduce-scatter.2.cloned.1.call-done = bf16[8,1024]{1,0:T(8,128)(2,1)} async-done(((bf16[8,4096]{1,0:T(8,128)(2,1)}), bf16[8,1024]{1,0:T(8,128)(2,1)}) %reduce-scatter.2.cloned.1.call-update) | async-done | bytes 16400 | tf_op jit(solution)/shard_map/reduce_scatter | solution.py:170
  188.6 9.0 %psum.55 = f32[8,1024]{1,0:T(8,128)S(1)} all-reduce(bf16[8,1024]{1,0:T(8,128)(2,1)} %reduce-scatter.2.cloned.1.call-done), channel_id=1, replica_groups=mesh['rep'=2,'seq'=4,'head'=2,'sub'=2] {'head'}, use_global_device_ids=true, to_apply=%region_15.16 | all-reduce | flops 8192 | bytes 49152 | tf_op jit(solution)/shard_map/psum | solution.py:173
  197.6 0.6 add_convert_fusion.1
  (65 shorter events, 0.9 us)
Async XLA Ops:
  7.2 4.0 %copy-start = (bf16[1024,512]{1,0:T(8,128)(2,1)S(1)}, bf16[1024,512]{1,0:T(8,128)(2,1)}, u32[]{:S(2)}) copy-start(bf16[1024,512]{1,0:T(8,128)(2,1)} %param.27) | copy-start | bytes 3145732
  7.2 3.8 %copy-start.6 = (bf16[8,1024]{1,0:T(8,128)(2,1)S(1)}, bf16[8,1024]{1,0:T(8,128)(2,1)}, u32[]{:S(2)}) copy-start(bf16[8,1024]{1,0:T(8,128)(2,1)} %param.24) | copy-start | bytes 49156
  7.2 4.0 %copy-start.10 = (f32[1024]{0:T(1024)S(1)}, f32[1024]{0:T(1024)}, u32[]{:S(2)}) copy-start(f32[1024]{0:T(1024)} %param.25) | copy-start | bytes 12292
  7.2 4.2 %copy-start.2 = (bf16[1024,512]{1,0:T(8,128)(2,1)S(1)}, bf16[1024,512]{1,0:T(8,128)(2,1)}, u32[]{:S(2)}) copy-start(bf16[1024,512]{1,0:T(8,128)(2,1)} %param.28) | copy-start | bytes 3145732
  7.2 4.5 %copy-start.16 = (s32[8]{0:T(128)S(1)}, s32[8]{0:T(128)}, u32[]{:S(2)}) copy-start(s32[8]{0:T(128)} %param.33) | copy-start | bytes 100
  7.2 26.0 %copy-start.8 = (f32[16,1024]{1,0:T(8,128)S(1)}, f32[16,1024]{1,0:T(8,128)}, u32[]{:S(2)}) copy-start(f32[16,1024]{1,0:T(8,128)} %param.42) | copy-start | bytes 196612
  7.2 26.0 %copy-start.15 = (s32[8]{0:T(128)S(1)}, s32[8]{0:T(128)}, u32[]{:S(2)}) copy-start(s32[8]{0:T(128)} %param.32) | copy-start | bytes 100
  7.2 41.0 %all-reduce.3.cloned.1.call-start = ((), (), s32[]{:S(2)}) async-start(), calls=%async_computation.1 | async-start | bytes 131072 | tf_op jit(solution)/shard_map/psum | solution.py:91
  11.0 177.7 %reduce-scatter.2.cloned.1.call-start = ((), (), s32[]{:S(2)}) async-start(), calls=%async_computation.2 | async-start | bytes 81920 | tf_op jit(solution)/shard_map/reduce_scatter | solution.py:170
  48.3 31.4 %copy-start.1 = (bf16[8,4,512,128]{3,2,1,0:T(8,128)(2,1)S(1)}, bf16[8,4,512,128]{3,2,1,0:T(8,128)(2,1)}, u32[]{:S(2)}) copy-start(bf16[8,4,512,128]{3,2,1,0:T(8,128)(2,1)} %param.31) | copy-start | bytes 12582916
  80.4 41.3 %copy-start.9 = (f32[4096]{0:T(1024)S(1)}, f32[4096]{0:T(1024)}, u32[]{:S(2)}) copy-start(f32[4096]{0:T(1024)} %param.34) | copy-start | bytes 49156
  121.7 4.8 %copy-start.7 = (f32[8,3,1024]{2,0,1:T(8,128)S(1)}, f32[8,3,1024]{2,0,1:T(8,128)}, u32[]{:S(2)}) copy-start(f32[8,3,1024]{2,0,1:T(8,128)} %param.38) | copy-start | bytes 294916
  121.7 4.8 %copy-start.12 = (f32[4,1024]{1,0:T(4,128)S(1)}, f32[4,1024]{1,0:T(4,128)}, u32[]{:S(2)}) copy-start(f32[4,1024]{1,0:T(4,128)} %param.36) | copy-start | bytes 49156
  121.7 4.8 %copy-start.3 = (bf16[1024,288]{0,1:T(8,128)(2,1)S(1)}, bf16[1024,288]{0,1:T(8,128)(2,1)}, u32[]{:S(2)}) copy-start(bf16[1024,288]{0,1:T(8,128)(2,1)} %param.39) | copy-start | bytes 1769476
  121.7 4.8 %copy-start.11 = (f32[1024]{0:T(1024)S(1)}, f32[1024]{0:T(1024)}, u32[]{:S(2)}) copy-start(f32[1024]{0:T(1024)} %param.37) | copy-start | bytes 12292
  121.7 40.2 %copy-start.5 = (bf16[256,1024]{1,0:T(8,128)(2,1)S(1)}, bf16[256,1024]{1,0:T(8,128)(2,1)}, u32[]{:S(2)}) copy-start(bf16[256,1024]{1,0:T(8,128)(2,1)} %param.40) | copy-start | bytes 1572868
  121.7 40.2 %copy-start.13 = (f32[1024]{0:T(1024)S(1)}, f32[1024]{0:T(1024)}, u32[]{:S(2)}) copy-start(f32[1024]{0:T(1024)} %param.41) | copy-start | bytes 12292
  121.7 40.4 %copy-start.4 = (f32[8,16,1024]{2,1,0:T(8,128)S(1)}, f32[8,16,1024]{2,1,0:T(8,128)}, u32[]{:S(2)}) copy-start(f32[8,16,1024]{2,1,0:T(8,128)} %param.44) | copy-start | bytes 1572868
  121.8 41.5 %copy-start.14 = (f32[1024]{0:T(1024)S(1)}, f32[1024]{0:T(1024)}, u32[]{:S(2)}) copy-start(f32[1024]{0:T(1024)} %param.43) | copy-start | bytes 12292
Sparse Core Ops, SparseCore 0:
  11.1 37.1 all-reduce.2
  172.1 16.4 reduce-scatter.1
where the time goes:
time: 205 us
  blocking collectives  127 us (62%)
  waiting for transfers between devices  31.3 us (15%)
  matrix products  25.4 us (12%)
  between operations  14.4 us (7%)
  other arithmetic  4.82 us (2%)
    all_gather x3, blocking collectives, joined(): pieces = jax.tree.map(lambda part: lax.all_gather(part, axis), value)  40.2 us
    psum x1, blocking collectives, local(): projected = lax.psum(proj_part, ('seq', 'head'))  35.1 us
    psum x1, blocking collectives, local(): sum_squares = lax.psum(squares, 'seq')  21.4 us
    reduce_scatter x1, waiting for transfers between devices, local(): lax.psum_scatter(mamba_part.astype(jnp.bfloat16), 'seq', scatter_dimensio...  16.6 us
    psum x1, waiting for transfers between devices, local(): lax.psum((part_query, part_key, part_value), 'seq')  14.7 us
    all_gather x1, blocking collectives, local(): full_tokens = lax.all_gather(mid_stream, 'seq', axis=1, tiled=True)  13.1 us
    psum x1, blocking collectives, local(): share = lax.psum(share, 'head')  8.99 us
    dot_general x1, matrix products, local(): mamba_part = jnp.dot(gated, w_mamba_out, preferred_element_type=jnp.float32)  8.73 us
  transfers between devices with their start and end apart: 2, of which 2 were waited for; matrix products, arithmetic and copies ran while one was open for 1% of the time, Pallas kernels for 0%

commit v1 on v0

--- a/solution.py
+++ b/solution.py
@@ -153,7 +153,7 @@
     mixed = jnp.sum(window * conv_weight[None, :, :], axis=1) + conv_bias[None, :]
     activated = jax.nn.silu(mixed)
     proj_part = jnp.dot(activated.astype(jnp.bfloat16), w_xproj, preferred_element_type=jnp.float32)
-    projected = lax.psum(proj_part, ("seq", "head"))
+    projected = lax.psum(lax.psum(proj_part, "head"), "seq")
     rank_width = w_dt.shape[0]
     state_width = ssm_state.shape[1]
     dt_low = projected[:, :rank_width].astype(jnp.bfloat16)

time: 205 us -> 196 us (0.956)
  blocking collectives: 127 us -> 117 us
    psum x1 -> x2, blocking collectives: 35.1 us -> 24.7 us  [local(): projected = lax.psum(lax.psum(proj_part, 'head'), 'seq')]
where the time goes in v1:
time: 196 us
  blocking collectives  117 us (60%)
  waiting for transfers between devices  32.3 us (16%)
  matrix products  25.4 us (13%)
  between operations  14.4 us (7%)
  other arithmetic  4.82 us (2%)
    all_gather x3, blocking collectives, joined(): pieces = jax.tree.map(lambda part: lax.all_gather(part, axis), value)  40.2 us
    psum x2, blocking collectives, local(): projected = lax.psum(lax.psum(proj_part, 'head'), 'seq')  24.7 us
    psum x1, blocking collectives, local(): sum_squares = lax.psum(squares, 'seq')  21.4 us
    reduce_scatter x1, waiting for transfers between devices, local(): lax.psum_scatter(mamba_part.astype(jnp.bfloat16), 'seq', scatter_dimensio...  17.6 us
    psum x1, waiting for transfers between devices, local(): lax.psum((part_query, part_key, part_value), 'seq')  14.7 us
    all_gather x1, blocking collectives, local(): full_tokens = lax.all_gather(mid_stream, 'seq', axis=1, tiled=True)  13.1 us
    psum x1, blocking collectives, local(): share = lax.psum(share, 'head')  8.93 us
    dot_general x1, matrix products, local(): mamba_part = jnp.dot(gated, w_mamba_out, preferred_element_type=jnp.float32)  8.73 us
  transfers between devices with their start and end apart: 2, of which 2 were waited for; matrix products, arithmetic and copies ran while one was open for 1% of the time, Pallas kernels for 0%

profile of v1, /device:TPU:0, one launch (start us, length us, event | category | flops | bytes accessed | tf_op | source)
XLA Modules:
  0.0 195.6 jit_solution(12998376942372014993)
XLA Ops:
  7.3 3.6 %fusion.46 = f32[8,2048]{1,0:T(8,128)} fusion(bf16[1024,2048]{1,0:T(8,128)(2,1)} %param.26, bf16[8,1024]{1,0:T(8,128)(2,1)} %param.24, f32[1024]{0:T(1024)} %param.25), kind=kOutput, calls=%fused_computation.68 | convolution fusion | flops 33579008 | bytes 4280320 | tf_op jit(solution)/shard_map/dot_general | solution.py:86
  11.0 0.1 fusion.25
  11.2 0.2 fusion.44
  11.4 0.2 fusion.42
  11.7 21.4 %all-reduce = (f32[8]{0:T(128)S(1)}, f32[8,512]{1,0:T(8,128)S(1)}, f32[8,512]{1,0:T(8,128)S(1)}) all-reduce(f32[8]{0:T(128)S(1)} %fusion.25, f32[8,512]{1,0:T(8,128)S(1)} %fusion.44, f32[8,512]{1,0:T(8,128)S(1)} %fusion.42), channel_id=1, replica_groups=mesh['rep'=2,'seq'=4,'head'=2,'sub'=2] {'seq'}, use_global_device_ids=true, to_apply=%region_2.0 | all-reduce | flops 8200 | bytes 65600 | tf_op jit(solution)/shard_map/psum | solution.py:90
  33.3 0.1 multiply_cosine_fusion
  33.6 14.7 %all-reduce.3.cloned.1.call-done = f32[8,2048]{1,0:T(8,128)} async-done(((f32[8,2048]{1,0:T(8,128)}), f32[8,2048]{1,0:T(8,128)}) %all-reduce.3.cloned.1.call-update) | async-done | bytes 65552 | tf_op jit(solution)/shard_map/psum | solution.py:91
  48.3 1.1 multiply_bitcast_fusion
  49.5 3.6 %select_reduce_fusion = (f32[8,4,4]{2,1,0:T(4,128)S(1)}, f32[8,4,4,512]{3,2,1,0:T(4,128)S(1)}) fusion(pred[8,512]{1,0:T(8,128)(4,1)S(1)} %broadcast_compare_fusion, bf16[8,4,512,128]{3,2,1,0:T(8,128)(2,1)} %param.30, bf16[8,4,4,64]{3,2,1,0:T(4,128)(2,1)S(1)} %bitcast.72, bf16[8,4,4,64]{3,2,1,0:T(4,128)(2,1)S(1)} %bitcast.70), kind=kOutput, calls=%fused_computation.21 | convolution fusion | flops 17039232 | bytes 4493824 | tf_op jit(solution)/shard_map/bhgd,bhtd->bhgt/dot_general | solution.py:105
  53.1 13.1 %all-gather = f32[32,4,4]{2,1,0:T(4,128)S(1)} all-gather(f32[8,4,4]{2,1,0:T(4,128)S(1)} %get-tuple-element.94), channel_id=2, replica_groups=mesh['rep'=2,'seq'=4,'head'=2,'sub'=2] {'seq'}, dimensions={0}, use_global_device_ids=true | all-gather | bytes 2560 | tf_op jit(solution)/shard_map/all_gather | solution.py:13
  66.2 0.3 fusion.13
  66.5 13.2 %all-gather.1 = f32[32,4,4]{2,1,0:T(4,128)S(1)} all-gather(f32[8,4,4]{2,1,0:T(4,128)S(1)} %fusion.13), channel_id=3, replica_groups=mesh['rep'=2,'seq'=4,'head'=2,'sub'=2] {'seq'}, dimensions={0}, use_global_device_ids=true | all-gather | bytes 2560 | tf_op jit(solution)/shard_map/all_gather | solution.py:13
  79.7 0.7 fusion.17
  80.4 13.9 %all-gather.2 = f32[32,4,4,128]{3,2,1,0:T(4,128)S(1)} all-gather(f32[8,4,4,128]{3,2,1,0:T(4,128)S(1)} %fusion.17), channel_id=4, replica_groups=mesh['rep'=2,'seq'=4,'head'=2,'sub'=2] {'seq'}, dimensions={0}, use_global_device_ids=true | all-gather | bytes 327680 | tf_op jit(solution)/shard_map/all_gather | solution.py:13
  94.3 0.2 fusion.37
  94.6 0.1 copy.59
  94.7 0.1 copy.50
  94.8 0.2 copy.52
  94.9 0.1 copy.51
  95.0 0.2 copy.53
  95.2 1.5 while.14
  95.2 0.1 copy.68
  95.3 0.1 copy.69
  95.4 0.2 fusion.73
  95.7 0.1 copy.68
  95.8 0.1 copy.69
  95.9 0.2 fusion.73
  96.2 0.1 copy.68
  96.3 0.1 copy.69
  96.4 0.2 fusion.73
  96.7 0.1 copy.57
  96.8 0.1 copy.54
  96.9 0.1 copy.55
  97.0 0.2 fusion.23
  97.2 2.8 %fusion.59 = f32[8,1024]{1,0:T(8,128)S(1)} fusion(bf16[8,2048]{1,0:T(8,128)(2,1)S(1)} %convert_element_type.78, bf16[2048,1024]{1,0:T(8,128)(2,1)} %param.29), kind=kOutput, calls=%fused_computation.88 | convolution fusion | flops 33554432 | bytes 4259840 | tf_op jit(solution)/shard_map/dot_general | solution.py:143
  100.0 8.3 %psum.60 = f32[8,1024]{1,0:T(8,128)S(1)} all-reduce(f32[8,1024]{1,0:T(8,128)S(1)} %fusion.59), channel_id=1, replica_groups=mesh['rep'=2,'seq'=4,'head'=2,'sub'=2] {'head'}, use_global_device_ids=true, to_apply=%region_9.10 | all-reduce | flops 8192 | bytes 65536 | tf_op jit(solution)/shard_map/psum | solution.py:144
  108.4 13.1 %all_gather.27 = bf16[8,4096]{1,0:T(8,128)(2,1)S(1)} all-gather(bf16[8,1024]{1,0:T(8,128)(2,1)S(1)} %fusion.26), channel_id=1, replica_groups=mesh['rep'=2,'seq'=4,'head'=2,'sub'=2] {'seq'}, dimensions={1}, use_global_device_ids=true | all-gather | bytes 81920 | tf_op jit(solution)/shard_map/all_gather | solution.py:146
  121.5 0.1 fusion.14
  121.8 4.7 %fusion.9 = f32[8,1,1024]{2,0,1:T(8,128)S(1)} fusion(bf16[2,4096,1024]{2,1,0:T(8,128)(2,1)} %param.35, bf16[8,4096]{1,0:T(8,128)(2,1)S(1)} %all_gather.27, f32[4096]{0:T(1024)S(1)} %copy-done.9, f32[8]{0:T(128)S(1)} %add_rsqrt_fusion), kind=kOutput, calls=%fused_computation.16 | convolution fusion | flops 67239936 | bytes 8503328 | tf_op jit(solution)/shard_map/dot_general | solution.py:150
  126.5 0.3 fusion.34
  126.8 7.1 %psum.61 = f32[8,288]{1,0:T(8,128)S(1)} all-reduce(f32[8,288]{1,0:T(8,128)S(1)} %fusion.34), channel_id=1, replica_groups=mesh['rep'=2,'seq'=4,'head'=2,'sub'=2] {'head'}, use_global_device_ids=true, to_apply=%region_12.13 | all-reduce | flops 2304 | bytes 18432 | tf_op jit(solution)/shard_map/psum | solution.py:156
  133.9 17.6 %psum.62 = f32[8,288]{1,0:T(8,128)S(1)} all-reduce(f32[8,288]{1,0:T(8,128)S(1)} %psum.61), channel_id=1, replica_groups=mesh['rep'=2,'seq'=4,'head'=2,'sub'=2] {'seq'}, use_global_device_ids=true, to_apply=%region_13.14 | all-reduce | flops 2304 | bytes 18432 | tf_op jit(solution)/shard_map/psum | solution.py:156
  151.6 0.2 fusion.54
  151.8 1.0 multiply_reduce_fusion
  152.9 8.7 %convolution_convert_fusion = bf16[8,4096]{1,0:T(8,128)(2,1)} fusion(bf16[1024,4096]{1,0:T(8,128)(2,1)} %param.45, bf16[2,4096,1024]{2,1,0:T(8,128)(2,1)} %param.35, f32[8,1024]{1,0:T(8,128)S(1)} %get-tuple-element.79, f32[1024]{0:T(1024)S(1)} %copy-done.14, bf16[8,4096]{1,0:T(8,128)(2,1)S(1)} %all_gather.27, f32[4096]{0:T(1024)S(1)} %copy-done.9, ...), kind=kOutput, calls=%fused_computation.14 | convolution fusion | flops 134488064 | bytes 16998432 | tf_op jit(solution)/shard_map/dot_general | solution.py:169
  161.6 17.6 %reduce-scatter.2.cloned.1.call-done = bf16[8,1024]{1,0:T(8,128)(2,1)} async-done(((bf16[8,4096]{1,0:T(8,128)(2,1)}), bf16[8,1024]{1,0:T(8,128)(2,1)}) %reduce-scatter.2.cloned.1.call-update) | async-done | bytes 16400 | tf_op jit(solution)/shard_map/reduce_scatter | solution.py:170
  179.2 8.9 %psum.63 = f32[8,1024]{1,0:T(8,128)S(1)} all-reduce(bf16[8,1024]{1,0:T(8,128)(2,1)} %reduce-scatter.2.cloned.1.call-done), channel_id=1, replica_groups=mesh['rep'=2,'seq'=4,'head'=2,'sub'=2] {'head'}, use_global_device_ids=true, to_apply=%region_16.17 | all-reduce | flops 8192 | bytes 49152 | tf_op jit(solution)/shard_map/psum | solution.py:173
  188.1 0.6 add_convert_fusion.1
  (66 shorter events, 0.9 us)
Async XLA Ops:
  7.2 4.0 %copy-start = (bf16[1024,512]{1,0:T(8,128)(2,1)S(1)}, bf16[1024,512]{1,0:T(8,128)(2,1)}, u32[]{:S(2)}) copy-start(bf16[1024,512]{1,0:T(8,128)(2,1)} %param.27) | copy-start | bytes 3145732
  7.2 3.8 %copy-start.6 = (bf16[8,1024]{1,0:T(8,128)(2,1)S(1)}, bf16[8,1024]{1,0:T(8,128)(2,1)}, u32[]{:S(2)}) copy-start(bf16[8,1024]{1,0:T(8,128)(2,1)} %param.24) | copy-start | bytes 49156
  7.2 4.0 %copy-start.10 = (f32[1024]{0:T(1024)S(1)}, f32[1024]{0:T(1024)}, u32[]{:S(2)}) copy-start(f32[1024]{0:T(1024)} %param.25) | copy-start | bytes 12292
  7.2 4.2 %copy-start.2 = (bf16[1024,512]{1,0:T(8,128)(2,1)S(1)}, bf16[1024,512]{1,0:T(8,128)(2,1)}, u32[]{:S(2)}) copy-start(bf16[1024,512]{1,0:T(8,128)(2,1)} %param.28) | copy-start | bytes 3145732
  7.2 4.5 %copy-start.16 = (s32[8]{0:T(128)S(1)}, s32[8]{0:T(128)}, u32[]{:S(2)}) copy-start(s32[8]{0:T(128)} %param.33) | copy-start | bytes 100
  7.2 26.0 %copy-start.8 = (f32[16,1024]{1,0:T(8,128)S(1)}, f32[16,1024]{1,0:T(8,128)}, u32[]{:S(2)}) copy-start(f32[16,1024]{1,0:T(8,128)} %param.42) | copy-start | bytes 196612
  7.2 26.0 %copy-start.15 = (s32[8]{0:T(128)S(1)}, s32[8]{0:T(128)}, u32[]{:S(2)}) copy-start(s32[8]{0:T(128)} %param.32) | copy-start | bytes 100
  7.2 41.0 %all-reduce.3.cloned.1.call-start = ((), (), s32[]{:S(2)}) async-start(), calls=%async_computation.1 | async-start | bytes 131072 | tf_op jit(solution)/shard_map/psum | solution.py:91
  11.0 168.2 %reduce-scatter.2.cloned.1.call-start = ((), (), s32[]{:S(2)}) async-start(), calls=%async_computation.2 | async-start | bytes 81920 | tf_op jit(solution)/shard_map/reduce_scatter | solution.py:170
  48.3 31.4 %copy-start.1 = (bf16[8,4,512,128]{3,2,1,0:T(8,128)(2,1)S(1)}, bf16[8,4,512,128]{3,2,1,0:T(8,128)(2,1)}, u32[]{:S(2)}) copy-start(bf16[8,4,512,128]{3,2,1,0:T(8,128)(2,1)} %param.31) | copy-start | bytes 12582916
  80.4 41.3 %copy-start.9 = (f32[4096]{0:T(1024)S(1)}, f32[4096]{0:T(1024)}, u32[]{:S(2)}) copy-start(f32[4096]{0:T(1024)} %param.34) | copy-start | bytes 49156
  121.7 4.8 %copy-start.7 = (f32[8,3,1024]{2,0,1:T(8,128)S(1)}, f32[8,3,1024]{2,0,1:T(8,128)}, u32[]{:S(2)}) copy-start(f32[8,3,1024]{2,0,1:T(8,128)} %param.38) | copy-start | bytes 294916
  121.7 4.8 %copy-start.12 = (f32[4,1024]{1,0:T(4,128)S(1)}, f32[4,1024]{1,0:T(4,128)}, u32[]{:S(2)}) copy-start(f32[4,1024]{1,0:T(4,128)} %param.36) | copy-start | bytes 49156
  121.7 4.8 %copy-start.3 = (bf16[1024,288]{0,1:T(8,128)(2,1)S(1)}, bf16[1024,288]{0,1:T(8,128)(2,1)}, u32[]{:S(2)}) copy-start(bf16[1024,288]{0,1:T(8,128)(2,1)} %param.39) | copy-start | bytes 1769476
  121.7 4.8 %copy-start.11 = (f32[1024]{0:T(1024)S(1)}, f32[1024]{0:T(1024)}, u32[]{:S(2)}) copy-start(f32[1024]{0:T(1024)} %param.37) | copy-start | bytes 12292
  121.7 29.9 %copy-start.5 = (bf16[256,1024]{1,0:T(8,128)(2,1)S(1)}, bf16[256,1024]{1,0:T(8,128)(2,1)}, u32[]{:S(2)}) copy-start(bf16[256,1024]{1,0:T(8,128)(2,1)} %param.40) | copy-start | bytes 1572868
  121.7 29.9 %copy-start.13 = (f32[1024]{0:T(1024)S(1)}, f32[1024]{0:T(1024)}, u32[]{:S(2)}) copy-start(f32[1024]{0:T(1024)} %param.41) | copy-start | bytes 12292
  121.7 30.1 %copy-start.4 = (f32[8,16,1024]{2,1,0:T(8,128)S(1)}, f32[8,16,1024]{2,1,0:T(8,128)}, u32[]{:S(2)}) copy-start(f32[8,16,1024]{2,1,0:T(8,128)} %param.44) | copy-start | bytes 1572868
  121.8 31.1 %copy-start.14 = (f32[1024]{0:T(1024)S(1)}, f32[1024]{0:T(1024)}, u32[]{:S(2)}) copy-start(f32[1024]{0:T(1024)} %param.43) | copy-start | bytes 12292
Sparse Core Ops, SparseCore 0:
  11.1 37.1 all-reduce.2
  161.8 17.3 reduce-scatter.1
